TPU v7x, 32 devices: a whole 2x2x4 slice. The times are simulated.
32 devices in a mesh: part: 4 (over x, y), fsdp: 8 (over z, core).
Axes of the slice: x: 2, y: 2, z: 4, core: 2. Of those that a mesh axis runs over, the one named last changes fastest.
Arguments:
- acts_in: bfloat16 [2, 65536, 768], P(None, ('part', 'fsdp')), parts along dimension 1
- cot_out: bfloat16 [2, 65536, 768], P(None, ('part', 'fsdp')), parts along dimension 1
- lengths: int32 [2, 32], P(None, ('part', 'fsdp')), parts along dimension 1
- w_up: bfloat16 [2, 768, 3072], replicated
- w_down: bfloat16 [2, 3072, 768], replicated
Outputs:
- output 1: float32 [8, 768, 3072], P('part', 'fsdp'), parts along dimension 0
- output 2: float32 [8, 3072, 768], P('part', 'fsdp'), parts along dimension 0
There are 4 independent parts. A program takes and returns all parts, laid end to end along the dimension named above; an argument that names none is the same for every part.
All inputs are finite; a program needn't handle non-finite values.
Results may differ from a plain program's by a relative error of at most 0.00977007.
Values are sent between devices in bfloat16 or wider.
A program may use at most 1 GiB of HBM per device.

v0:
```python
import functools

import jax
import jax.numpy as jnp
from jax import lax
from jax.experimental import pallas as pl
from jax.experimental.pallas import tpu as pltpu
from jax.sharding import PartitionSpec as P

MESH = pl.DeviceIdType.MESH
ANY = pl.BlockSpec(memory_space=pl.ANY)
F32 = jnp.float32
BF16 = jnp.bfloat16

C1 = 0.7978845608028654
K1 = C1 * 0.044715
K3 = 3.0 * K1

CHIPS = 4
SLOTS = 4
PIECES = 4


def dot(lhs, rhs, dims):
    return lax.dot_general(lhs, rhs, (dims, ((), ())), preferred_element_type=F32)


def gelu_parts(h_wide):
    sq = h_wide * h_wide
    th = jnp.tanh(h_wide * (C1 + K1 * sq))
    cdf = 0.5 + 0.5 * th
    return sq, th, cdf


def fwd_kernel(tiles, len_ref, x_ref, g_ref, w1_ref, w2_ref, x1_ref, r_ref, a_scr):
    step = pl.program_id(0)
    rows = x_ref.shape[0]
    left = len_ref[step // tiles] - (step % tiles) * rows
    row_ids = lax.broadcasted_iota(jnp.int32, r_ref.shape, 0)
    r_ref[...] = jnp.where(row_ids < left, g_ref[...], jnp.zeros_like(g_ref[...]))

    @pl.when(left > 0)
    def _():
        x_val = x_ref[...]
        width = w1_ref.shape[1] // 4
        for part in range(4):
            cols = slice(part * width, (part + 1) * width)
            h_val = dot(x_val, w1_ref[:, cols], ((1,), (0,))).astype(BF16).astype(F32)
            _, _, cdf = gelu_parts(h_val)
            a_scr[:, cols] = (h_val * cdf).astype(BF16)
        y_val = dot(a_scr[...], w2_ref[...], ((1,), (0,))).astype(BF16)
        x1_ref[...] = (x_val.astype(F32) + y_val.astype(F32)).astype(BF16)

    @pl.when(left <= 0)
    def _():
        x1_ref[...] = x_ref[...]


def forward(x0, g, lengths, w1, w2, micro, block):
    toks, dim = x0.shape
    ff = w1.shape[2]
    tiles = toks // micro // block
    tile_spec = pl.BlockSpec((block, dim), lambda i, n: (i, 0))
    return pl.pallas_call(
        functools.partial(fwd_kernel, tiles),
        out_shape=[jax.ShapeDtypeStruct((toks, dim), BF16)] * 2,
        grid_spec=pltpu.PrefetchScalarGridSpec(
            num_scalar_prefetch=1,
            grid=(toks // block,),
            in_specs=[
                tile_spec,
                tile_spec,
                pl.BlockSpec((None, dim, ff), lambda i, n: (0, 0, 0)),
                pl.BlockSpec((None, ff, dim), lambda i, n: (0, 0, 0)),
            ],
            out_specs=[tile_spec, tile_spec],
            scratch_shapes=[pltpu.VMEM((block, ff), BF16)],
        ),
        compiler_params=pltpu.CompilerParams(vmem_limit_bytes=58 * 1024 * 1024),
        name="fwd0",
    )(lengths, x0, g, w1, w2)


def grad_kernel(unit, block, x1_h, x0_h, r_h, wu_h, wd_h, gu_h, gd_h,
                xv, rv, dxa, slope_v, w1v, w2v, own_u, own_v, in_u, in_v, sum_u, sum_v,
                rr_u, rr_v, rl_u, rl_v, out_u, out_v,
                x_sem, r_sem, w_sem, ds_sem, dr_sem,
                rs_u, rq_u, ls_u, lq_u, rs_v, rq_v, ls_v, lq_v,
                ou_sem, ov_sem, du_credit, dv_credit, ru_credit, lu_credit, rv_credit, lv_credit):
    toks, dim = xv.shape
    layers, _, ff = wu_h.shape
    tiles = toks // block
    wide = 2 * unit
    per_dev = ff // (2 * CHIPS)
    per_layer = ff // wide
    total = layers * per_layer
    piece = unit // PIECES

    me = lax.axis_index("fsdp")
    z = me // 2
    core = me % 2
    peer = z * 2 + (1 - core)

    def signal(sem, dev):
        pl.semaphore_signal(sem, inc=1, device_id={"fsdp": dev}, device_id_type=MESH)

    barrier = pltpu.get_barrier_semaphore()
    signal(barrier, peer)

    @pl.when(z > 0)
    def _():
        signal(barrier, me - 2)

    @pl.when(z < CHIPS - 1)
    def _():
        signal(barrier, me + 2)

    def layer_of(m):
        return layers - 1 - m // per_layer

    def owner_of(m):
        return (1 + 3 * (m % per_layer)) % CHIPS

    def cols_of(m):
        base = 2 * per_dev * owner_of(m) + unit * ((m % per_layer) // CHIPS)
        return pl.multiple_of(base, unit), pl.multiple_of(base + per_dev, unit)

    def w_copies(m):
        slot = m % 2
        out = []
        for half, start in enumerate(cols_of(m)):
            span = pl.ds(start, unit)
            here = pl.ds(half * unit, unit)
            out.append(pltpu.make_async_copy(
                wu_h.at[layer_of(m), :, span], w1v.at[slot, :, here], w_sem.at[slot, half]))
            out.append(pltpu.make_async_copy(
                wd_h.at[layer_of(m), span, :], w2v.at[slot, here, :], w_sem.at[slot, 2 + half]))
        return out

    def rows_of(i):
        return pl.ds(pl.multiple_of(i * block, block), block)

    def x_copy(src, i):
        return pltpu.make_async_copy(src.at[rows_of(i), :], xv.at[rows_of(i), :], x_sem.at[i])

    def r_copy(i):
        return pltpu.make_async_copy(r_h.at[rows_of(i), :], rv.at[rows_of(i), :], r_sem.at[i])

    for cp in w_copies(0):
        cp.start()
    for i in range(tiles):
        x_copy(x1_h, i).start()
        r_copy(i).start()

    def clear(i, carry):
        dxa[rows_of(i), :] = jnp.zeros((block, dim), F32)
        return carry

    lax.fori_loop(0, tiles, clear, 0)
    peers = 1 + jnp.where(z > 0, 1, 0) + jnp.where(z < CHIPS - 1, 1, 0)
    pl.semaphore_wait(barrier, peers)

    def compute_v(m, back):
        own_v[...] = jnp.zeros(own_v.shape, F32)
        w1c = w1v.at[m % 2]

        def tile(i, carry):
            @pl.when(m % per_layer == 0)
            def _():
                x_copy(x1_h, i).wait()
                if back:
                    r_copy(i).wait()
                else:
                    rv[rows_of(i), :] = (rv[rows_of(i), :].astype(F32) + dxa[rows_of(i), :]).astype(BF16)

            h_val = dot(xv[rows_of(i), :], w1c[...], ((1,), (0,))).astype(BF16).astype(F32)
            sq, th, cdf = gelu_parts(h_val)
            a_val = (h_val * cdf).astype(BF16)
            slope_v[rows_of(i), :] = cdf + (h_val * (0.5 - 0.5 * (th * th))) * (C1 + K3 * sq)
            own_v[...] += dot(a_val, rv[rows_of(i), :], ((0,), (0,))).reshape(own_v.shape)
            return carry

        lax.fori_loop(0, tiles, tile, 0)

    def compute_u(m, back):
        own_u[...] = jnp.zeros(own_u.shape, F32)
        w1c = w1v.at[m % 2]
        w2c = w2v.at[m % 2]

        def tile(i, carry):
            da_val = dot(rv[rows_of(i), :], w2c[...], ((1,), (1,)))
            dh_val = (da_val * slope_v[rows_of(i), :]).astype(BF16)
            own_u[...] += dot(xv[rows_of(i), :], dh_val, ((0,), (0,))).reshape(own_u.shape)
            if back:
                dxa[rows_of(i), :] += dot(dh_val, w1c[...], ((1,), (1,)))
            return carry

        lax.fori_loop(0, tiles, tile, 0)

    def remote(src, dst, ssem, rsem, dev):
        return pltpu.make_async_remote_copy(
            src_ref=src, dst_ref=dst, send_sem=ssem, recv_sem=rsem,
            device_id={"fsdp": dev}, device_id_type=MESH)

    d_u = remote(own_u.at[:, 1 - core], in_u, ds_sem.at[0], dr_sem.at[0], peer)
    d_v = remote(own_v.at[1 - core], in_v, ds_sem.at[1], dr_sem.at[1], peer)

    def far_first(zz, going):
        return list(range(CHIPS - 1, zz, -1)) if going > 0 else list(range(zz))

    def u_copy(m, b, going, first):
        slot = m % SLOTS
        dst, ssem, qsem = (rr_u, rs_u, rq_u) if going > 0 else (rl_u, ls_u, lq_u)
        src = sum_u if first else dst
        return remote(src.at[slot, b], dst.at[slot, b], ssem.at[b, slot], qsem.at[b, slot], me + 2 * going)

    def v_copy(m, p, going, first):
        slot = m % SLOTS
        dst, ssem, qsem = (rr_v, rs_v, rq_v) if going > 0 else (rl_v, ls_v, lq_v)
        src = sum_v if first else dst
        part = pl.ds(p * piece, piece)
        return remote(src.at[slot, part], dst.at[slot, part], ssem.at[p, slot], qsem.at[p, slot], me + 2 * going)

    def beyond(m, zz, going):
        return owner_of(m) > zz if going > 0 else owner_of(m) < zz

    def ends(zz, going):
        start, stop = (0, CHIPS - 1) if going > 0 else (CHIPS - 1, 0)
        return zz == start, zz == stop

    def keeps(zz, going):
        dist = zz if going > 0 else CHIPS - 1 - zz
        return 2 * dist < CHIPS - 1

    def flow_u(m, zz, going):
        slot = m % SLOTS
        got, credit = (rr_u, ru_credit) if going > 0 else (rl_u, lu_credit)
        first, last = ends(zz, going)
        if not last:
            @pl.when(m >= SLOTS)
            def _():
                pl.semaphore_wait(credit, 1)

        for b in far_first(zz, going):
            if not first:
                u_copy(m, b, going, False).wait_recv()
                got[slot, b] += sum_u[slot, b]
            u_copy(m, b, going, first).start()
        if not first:
            u_copy(m, zz, going, False).wait_recv()
            if keeps(zz, going):
                got[slot, zz] += sum_u[slot, zz]

    def flow_v(m, zz, going):
        slot = m % SLOTS
        got, credit = (rr_v, rv_credit) if going > 0 else (rl_v, lv_credit)
        first, last = ends(zz, going)
        if not last:
            @pl.when(beyond(m, zz, going))
            def _():
                @pl.when(m >= SLOTS)
                def _():
                    pl.semaphore_wait(credit, 1)

                for p in range(PIECES):
                    if not first:
                        v_copy(m, p, going, False).wait_recv()
                        part = pl.ds(p * piece, piece)
                        got[slot, part] += sum_v[slot, part]
                    v_copy(m, p, going, first).start()

        if not first:
            @pl.when(owner_of(m) == zz)
            def _():
                for p in range(PIECES):
                    v_copy(m, p, going, False).wait_recv()
                if keeps(zz, going):
                    got[slot] += sum_v[slot]

    def out_copies_u(m):
        slot = m % 2
        return [
            pltpu.make_async_copy(out_u.at[slot, :, pl.ds(half * unit, unit)],
                                  gu_h.at[layer_of(m), :, pl.ds(start, unit)], ou_sem.at[slot, half])
            for half, start in enumerate(cols_of(m))
        ]

    def out_copy_v(m):
        start = pl.multiple_of(unit * ((m % per_layer) // CHIPS), unit)
        return pltpu.make_async_copy(out_v, gd_h.at[layer_of(m), pl.ds(start, unit), :], ov_sem)

    def terms(zz, total_ref, right_ref, left_ref):
        if zz == 0:
            return total_ref, left_ref
        if zz == CHIPS - 1:
            return total_ref, right_ref
        return right_ref, left_ref

    def finish_u(m, zz):
        slot = m % SLOTS

        @pl.when(m >= 2)
        def _():
            for cp in out_copies_u(m - 2):
                cp.wait()

        one, two = terms(zz, sum_u, rr_u, rl_u)
        out_u[m % 2] = one[slot, zz] + two[slot, zz]
        for cp in out_copies_u(m):
            cp.start()
        for going in (1, -1):
            for b in far_first(zz, going):
                u_copy(m, b, going, ends(zz, going)[0]).wait_send()

        @pl.when(m < total - SLOTS)
        def _():
            if zz > 0:
                signal(ru_credit, me - 2)
            if zz < CHIPS - 1:
                signal(lu_credit, me + 2)

    def finish_v(m, zz):
        slot = m % SLOTS

        @pl.when(owner_of(m) == zz)
        def _():
            @pl.when(m >= CHIPS)
            def _():
                out_copy_v(m - CHIPS).wait()

            one, two = terms(zz, sum_v, rr_v, rl_v)
            out_v[...] = one[slot] + two[slot]
            out_copy_v(m).start()

        for going in (1, -1):
            first, last = ends(zz, going)
            if not last:
                @pl.when(beyond(m, zz, going))
                def _():
                    for p in range(PIECES):
                        v_copy(m, p, going, first).wait_send()

            if not first:
                credit = rv_credit if going > 0 else lv_credit

                @pl.when(jnp.logical_and(beyond(m, zz - going, going), m < total - SLOTS))
                def _():
                    signal(credit, me - 2 * going)

    def live(m):
        return jnp.logical_and(m >= 0, m < total)

    def sums(t, lag, pair, mine, got, into, credit, flow, finish):
        m_core = t - lag

        @pl.when(live(m_core))
        def _():
            pair.wait_recv()
            into[m_core % SLOTS] = mine() + got[...]
            pair.wait_send()

            @pl.when(m_core < total - 1)
            def _():
                signal(credit, peer)

        for zz in range(CHIPS):
            @pl.when(z == zz)
            def _():
                for ahead, going in sorted([(zz, 1), (CHIPS - 1 - zz, -1)]):
                    m = t - lag - ahead

                    @pl.when(live(m))
                    def _():
                        flow(m, zz, going)

                m_end = t - lag - (CHIPS - 1)

                @pl.when(live(m_end))
                def _():
                    finish(m_end, zz)

    def send_pair(t, pair, credit):
        @pl.when(t > 0)
        def _():
            pl.semaphore_wait(credit, 1)

        pair.start()

    def iteration(t, carry):
        back = t < per_layer
        front = jnp.logical_and(t >= per_layer, t < total)

        @pl.when(t < total)
        def _():
            @pl.when(t + 1 < total)
            def _():
                for cp in w_copies(t + 1):
                    cp.start()

            for cp in w_copies(t):
                cp.wait()

            @pl.when(t == per_layer)
            def _():
                for i in range(tiles):
                    x_copy(x0_h, i).start()

        @pl.when(back)
        def _():
            compute_v(t, True)

        @pl.when(front)
        def _():
            compute_v(t, False)

        @pl.when(t < total)
        def _():
            send_pair(t, d_v, dv_credit)

        sums(t, 1, d_u, lambda: own_u[:, core], in_u, sum_u, du_credit, flow_u, finish_u)

        @pl.when(back)
        def _():
            compute_u(t, True)

        @pl.when(front)
        def _():
            compute_u(t, False)

        @pl.when(t < total)
        def _():
            send_pair(t, d_u, du_credit)

        sums(t, 0, d_v, lambda: own_v[core], in_v, sum_v, dv_credit, flow_v, finish_v)
        return carry

    lax.fori_loop(0, total + CHIPS, iteration, 0)

    for m in (total - 2, total - 1):
        for cp in out_copies_u(m):
            cp.wait()
    out_copy_v(total - CHIPS).wait()


def gradients(x1, x0, r, w_up, w_down, block, unit):
    toks, dim = x0.shape
    layers, _, ff = w_up.shape
    rows_u = dim // (2 * CHIPS)
    wide = 2 * unit
    tiles = toks // block
    dma = pltpu.SemaphoreType.DMA
    vm = pltpu.VMEM
    u_blk = (CHIPS, rows_u, wide)
    v_blk = (unit, dim)
    line_sems = [dma((CHIPS, SLOTS))] * 4 + [dma((PIECES, SLOTS))] * 4
    scratch = [
        vm((toks, dim), BF16), vm((toks, dim), BF16), vm((toks, dim), F32), vm((toks, wide), F32),
        vm((2, dim, wide), BF16), vm((2, wide, dim), BF16),
        vm((CHIPS, 2, rows_u, wide), F32), vm((2,) + v_blk, F32),
        vm(u_blk, F32), vm(v_blk, F32),
        vm((SLOTS,) + u_blk, F32), vm((SLOTS,) + v_blk, F32),
        vm((SLOTS,) + u_blk, F32), vm((SLOTS,) + v_blk, F32),
        vm((SLOTS,) + u_blk, F32), vm((SLOTS,) + v_blk, F32),
        vm((2, rows_u, wide), F32), vm(v_blk, F32),
        dma((tiles,)), dma((tiles,)), dma((2, 4)), dma((2,)), dma((2,)),
        *line_sems,
        dma((2, 2)), dma,
    ] + [pltpu.SemaphoreType.REGULAR] * 6
    return pl.pallas_call(
        functools.partial(grad_kernel, unit, block),
        out_shape=[
            jax.ShapeDtypeStruct((layers, rows_u, ff), F32),
            jax.ShapeDtypeStruct((layers, ff // (2 * CHIPS), dim), F32),
        ],
        in_specs=[ANY] * 5,
        out_specs=[ANY] * 2,
        scratch_shapes=scratch,
        compiler_params=pltpu.CompilerParams(
            collective_id=0, has_side_effects=True, vmem_limit_bytes=62 * 1024 * 1024),
        name="grads",
    )(x1, x0, r, w_up, w_down)


def solution(mesh, block=512, unit=128):
    def local_step(acts_in, cot_out, lengths, w_up, w_down):
        micro, tok_rows, dim = acts_in.shape
        x0 = acts_in.reshape(micro * tok_rows, dim)
        g = cot_out.reshape(micro * tok_rows, dim)
        x1, r = forward(x0, g, lengths.reshape(micro), w_up, w_down, micro, block)
        return gradients(x1, x0, r, w_up, w_down, block, unit)

    act_spec = P(None, ("part", "fsdp"), None)
    grad_spec = P("part", "fsdp", None)
    return jax.shard_map(
        local_step, mesh=mesh,
        in_specs=(act_spec, act_spec, P(None, ("part", "fsdp")), P(), P()),
        out_specs=(grad_spec, grad_spec), check_vma=False)
```

profile of v0, /device:TPU:16, one launch (start us, length us, event | category | flops | bytes accessed | tf_op | source)
XLA Modules:
  0.0 556.5 jit_solution(8693909664109280765)
XLA Ops:
  0.6 40.9 %fwd0.1 = (bf16[4096,768]{1,0:T(8,128)(2,1)}, bf16[4096,768]{1,0:T(8,128)(2,1)}) custom-call(s32[2]{0:T(128)} %bitcast.6, bf16[4096,768]{1,0:T(8,128)(2,1)} %bitcast.3, bf16[4096,768]{1,0:T(8,128)(2,1)} %bitcast.5, bf16[2,768,3072]{2,1,0:T(8,128)(2,1)} %wu_h.1, bf16[2,3072,768]{2,1,0:T(8,128)(2,1)} %wd_h.1), custom_call_target="tpu_custom_call" | custom-call | tf_op jit(solution)/shard_map/fwd0/pallas_call | solution.py:64
  41.5 510.1 %grads.1 = (f32[2,96,3072]{2,1,0:T(8,128)}, f32[2,384,768]{2,1,0:T(8,128)}) custom-call(bf16[4096,768]{1,0:T(8,128)(2,1)} %get-tuple-element.4.x1_h, bf16[4096,768]{1,0:T(8,128)(2,1)} %bitcast.4, bf16[4096,768]{1,0:T(8,128)(2,1)} %get-tuple-element.5.r_h, bf16[2,768,3072]{2,1,0:T(8,128)(2,1)} %wu_h.1, bf16[2,3072,768]{2,1,0:T(8,128)(2,1)} %wd_h.1), custom_call_target="tpu_custom_call" | custom-call | tf_op jit(solution)/shard_map/grads/pallas_call | solution.py:469
  551.6 0.0 copy-start
  551.6 3.4 copy.9
  555.1 0.0 copy-done
  555.1 1.4 copy.10
Async XLA Ops:
  551.6 3.5 copy-start
where the time goes:
time: 560 us; the launch traced here: 556 us
  Pallas kernels  551 us (98%)
    pallas_call x1, Pallas kernels, gradients(): pl.pallas_call(functools.partial(grad_kernel, unit, block), out_shape=[ja...  510 us
    pallas_call x1, Pallas kernels, forward(): pl.pallas_call(functools.partial(fwd_kernel, tiles), out_shape=[jax.Shape...  40.9 us

commit v1 on v0

--- a/solution.py
+++ b/solution.py
@@ -18,7 +18,7 @@
 
 CHIPS = 4
 SLOTS = 4
-PIECES = 4
+WSLOTS = 3
 
 
 def dot(lhs, rhs, dims):
@@ -30,6 +30,12 @@
     th = jnp.tanh(h_wide * (C1 + K1 * sq))
     cdf = 0.5 + 0.5 * th
     return sq, th, cdf
+
+
+def gelu_pair(h_wide):
+    sq, th, cdf = gelu_parts(h_wide)
+    slope = cdf + (h_wide * (0.5 - 0.5 * (th * th))) * (C1 + K3 * sq)
+    return (h_wide * cdf).astype(BF16), slope
 
 
 def fwd_kernel(tiles, len_ref, x_ref, g_ref, w1_ref, w2_ref, x1_ref, r_ref, a_scr):
@@ -94,7 +100,8 @@
     per_dev = ff // (2 * CHIPS)
     per_layer = ff // wide
     total = layers * per_layer
-    piece = unit // PIECES
+    switch = per_layer + 2
+    last_step = total + 2
 
     me = lax.axis_index("fsdp")
     z = me // 2
@@ -126,7 +133,7 @@
         return pl.multiple_of(base, unit), pl.multiple_of(base + per_dev, unit)
 
     def w_copies(m):
-        slot = m % 2
+        slot = m % WSLOTS
         out = []
         for half, start in enumerate(cols_of(m)):
             span = pl.ds(start, unit)
@@ -160,66 +167,66 @@
     peers = 1 + jnp.where(z > 0, 1, 0) + jnp.where(z < CHIPS - 1, 1, 0)
     pl.semaphore_wait(barrier, peers)
 
-    def compute_v(m, back):
-        own_v[...] = jnp.zeros(own_v.shape, F32)
-        w1c = w1v.at[m % 2]
-
-        def tile(i, carry):
-            @pl.when(m % per_layer == 0)
-            def _():
-                x_copy(x1_h, i).wait()
-                if back:
-                    r_copy(i).wait()
-                else:
-                    rv[rows_of(i), :] = (rv[rows_of(i), :].astype(F32) + dxa[rows_of(i), :]).astype(BF16)
-
-            h_val = dot(xv[rows_of(i), :], w1c[...], ((1,), (0,))).astype(BF16).astype(F32)
-            sq, th, cdf = gelu_parts(h_val)
-            a_val = (h_val * cdf).astype(BF16)
-            slope_v[rows_of(i), :] = cdf + (h_val * (0.5 - 0.5 * (th * th))) * (C1 + K3 * sq)
-            own_v[...] += dot(a_val, rv[rows_of(i), :], ((0,), (0,))).reshape(own_v.shape)
-            return carry
-
-        lax.fori_loop(0, tiles, tile, 0)
-
-    def compute_u(m, back):
-        own_u[...] = jnp.zeros(own_u.shape, F32)
-        w1c = w1v.at[m % 2]
-        w2c = w2v.at[m % 2]
-
-        def tile(i, carry):
-            da_val = dot(rv[rows_of(i), :], w2c[...], ((1,), (1,)))
-            dh_val = (da_val * slope_v[rows_of(i), :]).astype(BF16)
-            own_u[...] += dot(xv[rows_of(i), :], dh_val, ((0,), (0,))).reshape(own_u.shape)
-            if back:
-                dxa[rows_of(i), :] += dot(dh_val, w1c[...], ((1,), (1,)))
-            return carry
-
-        lax.fori_loop(0, tiles, tile, 0)
+    def v_tile(m, i):
+        h_val = dot(xv[rows_of(i), :], w1v[m % WSLOTS], ((1,), (0,))).astype(BF16).astype(F32)
+        a_val, slope_v[rows_of(i), :] = gelu_pair(h_val)
+        own_v[m % 2] += dot(a_val, rv[rows_of(i), :], ((0,), (0,))).reshape(own_v.shape[1:])
+
+    def u_tile(m, i, back):
+        da_val = dot(rv[rows_of(i), :], w2v[m % WSLOTS], ((1,), (1,)))
+        dh_val = (da_val * slope_v[rows_of(i), :]).astype(BF16)
+        own_u[m % 2] += dot(xv[rows_of(i), :], dh_val, ((0,), (0,))).reshape(own_u.shape[1:])
+        if back:
+            dxa[rows_of(i), :] += dot(dh_val, w1v[m % WSLOTS], ((1,), (1,)))
+
+    def both_tile(mv, mu, i, back):
+        rows = rows_of(i)
+        x_i, r_i = xv[rows, :], rv[rows, :]
+        da_val = dot(r_i, w2v[mu % WSLOTS], ((1,), (1,)))
+        dh_val = (da_val * slope_v[rows, :]).astype(BF16)
+        h_val = dot(x_i, w1v[mv % WSLOTS], ((1,), (0,))).astype(BF16).astype(F32)
+        if back:
+            dxa[rows, :] += dot(dh_val, w1v[mu % WSLOTS], ((1,), (1,)))
+        a_val, slope_v[rows, :] = gelu_pair(h_val)
+        own_u[mu % 2] += dot(x_i, dh_val, ((0,), (0,))).reshape(own_u.shape[1:])
+        own_v[mv % 2] += dot(a_val, r_i, ((0,), (0,))).reshape(own_v.shape[1:])
+
+    def arrive(n, i):
+        @pl.when(n == 0)
+        def _():
+            x_copy(x1_h, i).wait()
+            r_copy(i).wait()
+
+        @pl.when(n == switch)
+        def _():
+            x_copy(x0_h, i).wait()
+            rv[rows_of(i), :] = (rv[rows_of(i), :].astype(F32) + dxa[rows_of(i), :]).astype(BF16)
 
     def remote(src, dst, ssem, rsem, dev):
         return pltpu.make_async_remote_copy(
             src_ref=src, dst_ref=dst, send_sem=ssem, recv_sem=rsem,
             device_id={"fsdp": dev}, device_id_type=MESH)
 
-    d_u = remote(own_u.at[:, 1 - core], in_u, ds_sem.at[0], dr_sem.at[0], peer)
-    d_v = remote(own_v.at[1 - core], in_v, ds_sem.at[1], dr_sem.at[1], peer)
-
-    def far_first(zz, going):
-        return list(range(CHIPS - 1, zz, -1)) if going > 0 else list(range(zz))
-
-    def u_copy(m, b, going, first):
+    def d_u(m):
+        slot = m % 2
+        return remote(own_u.at[slot, :, 1 - core], in_u.at[slot], ds_sem.at[0, slot], dr_sem.at[0, slot], peer)
+
+    def d_v(m):
+        slot = m % 2
+        return remote(own_v.at[slot, 1 - core], in_v.at[slot], ds_sem.at[1, slot], dr_sem.at[1, slot], peer)
+
+    def u_copy(m, zz, going, first):
         slot = m % SLOTS
         dst, ssem, qsem = (rr_u, rs_u, rq_u) if going > 0 else (rl_u, ls_u, lq_u)
         src = sum_u if first else dst
-        return remote(src.at[slot, b], dst.at[slot, b], ssem.at[b, slot], qsem.at[b, slot], me + 2 * going)
-
-    def v_copy(m, p, going, first):
+        part = pl.ds(zz + 1, CHIPS - 1 - zz) if going > 0 else pl.ds(0, zz)
+        return remote(src.at[slot, part], dst.at[slot, part], ssem.at[slot], qsem.at[slot], me + 2 * going)
+
+    def v_copy(m, going, first):
         slot = m % SLOTS
         dst, ssem, qsem = (rr_v, rs_v, rq_v) if going > 0 else (rl_v, ls_v, lq_v)
         src = sum_v if first else dst
-        part = pl.ds(p * piece, piece)
-        return remote(src.at[slot, part], dst.at[slot, part], ssem.at[p, slot], qsem.at[p, slot], me + 2 * going)
+        return remote(src.at[slot], dst.at[slot], ssem.at[slot], qsem.at[slot], me + 2 * going)
 
     def beyond(m, zz, going):
         return owner_of(m) > zz if going > 0 else owner_of(m) < zz
@@ -236,25 +243,32 @@
         slot = m % SLOTS
         got, credit = (rr_u, ru_credit) if going > 0 else (rl_u, lu_credit)
         first, last = ends(zz, going)
+        if not first:
+            u_copy(m, zz - going, going, False).wait_recv()
+            near = zz if keeps(zz, going) else zz + going
+            lo, hi = (near, CHIPS) if going > 0 else (0, near + 1)
+            if hi > lo:
+                got[slot, lo:hi] += sum_u[slot, lo:hi]
         if not last:
             @pl.when(m >= SLOTS)
             def _():
                 pl.semaphore_wait(credit, 1)
 
-        for b in far_first(zz, going):
-            if not first:
-                u_copy(m, b, going, False).wait_recv()
-                got[slot, b] += sum_u[slot, b]
-            u_copy(m, b, going, first).start()
-        if not first:
-            u_copy(m, zz, going, False).wait_recv()
-            if keeps(zz, going):
-                got[slot, zz] += sum_u[slot, zz]
+            u_copy(m, zz, going, first).start()
 
     def flow_v(m, zz, going):
         slot = m % SLOTS
         got, credit = (rr_v, rv_credit) if going > 0 else (rl_v, lv_credit)
         first, last = ends(zz, going)
+        if not first:
+            @pl.when(beyond(m, zz - going, going))
+            def _():
+                v_copy(m, going, False).wait_recv()
+
+            @pl.when(beyond(m, zz - going if keeps(zz, going) else zz, going))
+            def _():
+                got[slot] += sum_v[slot]
+
         if not last:
             @pl.when(beyond(m, zz, going))
             def _():
@@ -262,20 +276,7 @@
                 def _():
                     pl.semaphore_wait(credit, 1)
 
-                for p in range(PIECES):
-                    if not first:
-                        v_copy(m, p, going, False).wait_recv()
-                        part = pl.ds(p * piece, piece)
-                        got[slot, part] += sum_v[slot, part]
-                    v_copy(m, p, going, first).start()
-
-        if not first:
-            @pl.when(owner_of(m) == zz)
-            def _():
-                for p in range(PIECES):
-                    v_copy(m, p, going, False).wait_recv()
-                if keeps(zz, going):
-                    got[slot] += sum_v[slot]
+                v_copy(m, going, first).start()
 
     def out_copies_u(m):
         slot = m % 2
@@ -309,8 +310,9 @@
         for cp in out_copies_u(m):
             cp.start()
         for going in (1, -1):
-            for b in far_first(zz, going):
-                u_copy(m, b, going, ends(zz, going)[0]).wait_send()
+            first, last = ends(zz, going)
+            if not last:
+                u_copy(m, zz, going, first).wait_send()
 
         @pl.when(m < total - SLOTS)
         def _():
@@ -337,8 +339,7 @@
             if not last:
                 @pl.when(beyond(m, zz, going))
                 def _():
-                    for p in range(PIECES):
-                        v_copy(m, p, going, first).wait_send()
+                    v_copy(m, going, first).wait_send()
 
             if not first:
                 credit = rv_credit if going > 0 else lv_credit
@@ -347,19 +348,26 @@
                 def _():
                     signal(credit, me - 2 * going)
 
-    def live(m):
-        return jnp.logical_and(m >= 0, m < total)
-
-    def sums(t, lag, pair, mine, got, into, credit, flow, finish):
-        m_core = t - lag
-
-        @pl.when(live(m_core))
-        def _():
-            pair.wait_recv()
-            into[m_core % SLOTS] = mine() + got[...]
-            pair.wait_send()
-
-            @pl.when(m_core < total - 1)
+    def v_of(n):
+        m = jnp.where(n == 0, 0, jnp.where(n < switch, n - 1, n - 2))
+        none = (n < 0) | (n == 1) | (n == switch - 1) | (n >= last_step)
+        return jnp.where(none, -1, m)
+
+    def u_of(n):
+        m = jnp.where(n == 1, 0, jnp.where(n < switch, n - 2, n - 3))
+        none = (n < 1) | (n == 2) | (n == switch) | (n > last_step)
+        return jnp.where(none, -1, m)
+
+    def sums(n, index, pair, mine, got, into, credit, flow, finish):
+        m_core = index(n - 1)
+
+        @pl.when(m_core >= 0)
+        def _():
+            pair(m_core).wait_recv()
+            into[m_core % SLOTS] = mine(m_core % 2) + got[m_core % 2]
+            pair(m_core).wait_send()
+
+            @pl.when(m_core < total - 2)
             def _():
                 signal(credit, peer)
 
@@ -367,74 +375,107 @@
             @pl.when(z == zz)
             def _():
                 for ahead, going in sorted([(zz, 1), (CHIPS - 1 - zz, -1)]):
-                    m = t - lag - ahead
-
-                    @pl.when(live(m))
+                    m = index(n - 1 - ahead)
+
+                    @pl.when(m >= 0)
                     def _():
                         flow(m, zz, going)
 
-                m_end = t - lag - (CHIPS - 1)
-
-                @pl.when(live(m_end))
+                m_end = index(n - CHIPS)
+
+                @pl.when(m_end >= 0)
                 def _():
                     finish(m_end, zz)
 
-    def send_pair(t, pair, credit):
-        @pl.when(t > 0)
-        def _():
-            pl.semaphore_wait(credit, 1)
-
-        pair.start()
-
-    def iteration(t, carry):
-        back = t < per_layer
-        front = jnp.logical_and(t >= per_layer, t < total)
-
-        @pl.when(t < total)
-        def _():
-            @pl.when(t + 1 < total)
-            def _():
-                for cp in w_copies(t + 1):
+    def all_sums(n):
+        sums(n, v_of, d_v, lambda slot: own_v[slot, core], in_v, sum_v, dv_credit, flow_v, finish_v)
+        sums(n, u_of, d_u, lambda slot: own_u[slot, :, core], in_u, sum_u, du_credit, flow_u, finish_u)
+
+    def step(n, carry):
+        mv, mu = v_of(n), u_of(n)
+        has_v, has_u = mv >= 0, mu >= 0
+        both = has_v & has_u
+        back = n < switch
+
+        @pl.when(has_v)
+        def _():
+            @pl.when(mv + 1 < total)
+            def _():
+                for cp in w_copies(mv + 1):
                     cp.start()
 
-            for cp in w_copies(t):
+            for cp in w_copies(mv):
                 cp.wait()
 
-            @pl.when(t == per_layer)
-            def _():
-                for i in range(tiles):
-                    x_copy(x0_h, i).start()
-
-        @pl.when(back)
-        def _():
-            compute_v(t, True)
-
-        @pl.when(front)
-        def _():
-            compute_v(t, False)
-
-        @pl.when(t < total)
-        def _():
-            send_pair(t, d_v, dv_credit)
-
-        sums(t, 1, d_u, lambda: own_u[:, core], in_u, sum_u, du_credit, flow_u, finish_u)
-
-        @pl.when(back)
-        def _():
-            compute_u(t, True)
-
-        @pl.when(front)
-        def _():
-            compute_u(t, False)
-
-        @pl.when(t < total)
-        def _():
-            send_pair(t, d_u, du_credit)
-
-        sums(t, 0, d_v, lambda: own_v[core], in_v, sum_v, dv_credit, flow_v, finish_v)
+        @pl.when(n == switch)
+        def _():
+            for i in range(tiles):
+                x_copy(x0_h, i).start()
+
+        @pl.when(has_v)
+        def _():
+            own_v[mv % 2] = jnp.zeros(own_v.shape[1:], F32)
+
+        @pl.when(has_u)
+        def _():
+            own_u[mu % 2] = jnp.zeros(own_u.shape[1:], F32)
+
+        early = jnp.where(n == 1, 0, tiles // 4)
+
+        def half(phase, c):
+            lo = jnp.where(phase == 0, 0, early)
+            hi = jnp.where(phase == 0, early, tiles)
+
+            def loop(cond, body):
+                @pl.when(cond)
+                def _():
+                    lax.fori_loop(lo, hi, body, 0)
+
+            def v_body(i, c):
+                arrive(n, i)
+                v_tile(mv, i)
+                return c
+
+            def u_body(is_back):
+                def body(i, c):
+                    u_tile(mu, i, is_back)
+                    return c
+                return body
+
+            def both_body(is_back):
+                def body(i, c):
+                    both_tile(mv, mu, i, is_back)
+                    return c
+                return body
+
+            loop(has_v & ~has_u, v_body)
+            loop(has_u & ~has_v & back, u_body(True))
+            loop(has_u & ~has_v & ~back, u_body(False))
+            loop(both & back, both_body(True))
+            loop(both & ~back, both_body(False))
+
+            @pl.when(phase == 0)
+            def _():
+                all_sums(n)
+
+            return c
+
+        lax.fori_loop(0, 2, half, 0)
+
+        def send_pair(m, pair, credit):
+            @pl.when(m >= 0)
+            def _():
+                @pl.when(m >= 2)
+                def _():
+                    pl.semaphore_wait(credit, 1)
+
+                pair(m).start()
+
+        send_pair(mv, d_v, dv_credit)
+        send_pair(mu, d_u, du_credit)
         return carry
 
-    lax.fori_loop(0, total + CHIPS, iteration, 0)
+    lax.fori_loop(0, last_step + CHIPS + 1, step, 0)
 
     for m in (total - 2, total - 1):
         for cp in out_copies_u(m):
@@ -452,20 +493,17 @@
     vm = pltpu.VMEM
     u_blk = (CHIPS, rows_u, wide)
     v_blk = (unit, dim)
-    line_sems = [dma((CHIPS, SLOTS))] * 4 + [dma((PIECES, SLOTS))] * 4
     scratch = [
         vm((toks, dim), BF16), vm((toks, dim), BF16), vm((toks, dim), F32), vm((toks, wide), F32),
-        vm((2, dim, wide), BF16), vm((2, wide, dim), BF16),
-        vm((CHIPS, 2, rows_u, wide), F32), vm((2,) + v_blk, F32),
-        vm(u_blk, F32), vm(v_blk, F32),
+        vm((WSLOTS, dim, wide), BF16), vm((WSLOTS, wide, dim), BF16),
+        vm((2, CHIPS, 2, rows_u, wide), F32), vm((2, 2) + v_blk, F32),
+        vm((2,) + u_blk, F32), vm((2,) + v_blk, F32),
         vm((SLOTS,) + u_blk, F32), vm((SLOTS,) + v_blk, F32),
         vm((SLOTS,) + u_blk, F32), vm((SLOTS,) + v_blk, F32),
         vm((SLOTS,) + u_blk, F32), vm((SLOTS,) + v_blk, F32),
         vm((2, rows_u, wide), F32), vm(v_blk, F32),
-        dma((tiles,)), dma((tiles,)), dma((2, 4)), dma((2,)), dma((2,)),
-        *line_sems,
-        dma((2, 2)), dma,
-    ] + [pltpu.SemaphoreType.REGULAR] * 6
+        dma((tiles,)), dma((tiles,)), dma((WSLOTS, 4)), dma((2, 2)), dma((2, 2)),
+    ] + [dma((SLOTS,))] * 8 + [dma((2, 2)), dma] + [pltpu.SemaphoreType.REGULAR] * 6
     return pl.pallas_call(
         functools.partial(grad_kernel, unit, block),
         out_shape=[

time: 560 us -> 428 us (0.76)
  Pallas kernels: 551 us -> 415 us
    pallas_call x1, Pallas kernels: 510 us -> 377 us  [gradients(): pl.pallas_call(functools.partial(grad_kernel, unit, block), out_shape=[ja...]
where the time goes in v1:
time: 428 us; the launch traced here: 421 us
  Pallas kernels  415 us (97%)
  local copies, waits for them, and re-layouts  4.86 us (1%)
    pallas_call x1, Pallas kernels, gradients(): pl.pallas_call(functools.partial(grad_kernel, unit, block), out_shape=[ja...  377 us
    pallas_call x1, Pallas kernels, forward(): pl.pallas_call(functools.partial(fwd_kernel, tiles), out_shape=[jax.Shape...  38 us

profile of v1, /device:TPU:16, one launch (start us, length us, event | category | flops | bytes accessed | tf_op | source)
XLA Modules:
  0.0 421.0 jit_solution(10742896388960435179)
XLA Ops:
  0.6 38.0 %fwd0.1 = (bf16[4096,768]{1,0:T(8,128)(2,1)}, bf16[4096,768]{1,0:T(8,128)(2,1)}) custom-call(s32[2]{0:T(128)} %bitcast.6, bf16[4096,768]{1,0:T(8,128)(2,1)} %bitcast.3, bf16[4096,768]{1,0:T(8,128)(2,1)} %bitcast.5, bf16[2,768,3072]{2,1,0:T(8,128)(2,1)} %wu_h.1, bf16[2,3072,768]{2,1,0:T(8,128)(2,1)} %wd_h.1), custom_call_target="tpu_custom_call" | custom-call | tf_op jit(solution)/shard_map/fwd0/pallas_call | solution.py:70
  38.6 377.5 %grads.1 = (f32[2,96,3072]{2,1,0:T(8,128)}, f32[2,384,768]{2,1,0:T(8,128)}) custom-call(bf16[4096,768]{1,0:T(8,128)(2,1)} %get-tuple-element.4.x1_h, bf16[4096,768]{1,0:T(8,128)(2,1)} %bitcast.4, bf16[4096,768]{1,0:T(8,128)(2,1)} %get-tuple-element.5.r_h, bf16[2,768,3072]{2,1,0:T(8,128)(2,1)} %wu_h.1, bf16[2,3072,768]{2,1,0:T(8,128)(2,1)} %wd_h.1), custom_call_target="tpu_custom_call" | custom-call | tf_op jit(solution)/shard_map/grads/pallas_call | solution.py:507
  416.1 0.0 copy-start
  416.1 3.4 copy.9
  419.6 0.0 copy-done
  419.6 1.4 copy.10
Async XLA Ops:
  416.1 3.5 copy-start
